TPU v7x, 32 devices: a whole 2x2x4 slice. The times are simulated.
32 devices in a mesh: ka: 8 (over z, y), ga: 4 (over x, core).
Axes of the slice: x: 2, y: 2, z: 4, core: 2. Of those that a mesh axis runs over, the one named last changes fastest.
Arguments:
- x_dens: bfloat16 [32, 64, 1500], P('ka', None, 'ga'), may hold values from -6 to 6
- y_dens: bfloat16 [32, 64, 1500], P('ka', None, 'ga'), may hold values from -0.15625 to 0.15625
- p_dens: bfloat16 [32, 64, 1500], P('ka', None, 'ga'), may hold values from -1 to 1
- coulomb: float32 [1500], P('ga'), may hold values from 0.1 to 2
- screened: bfloat16 [16, 1500, 1500], P('ka', 'ga'), may hold values from -0.15625 to 0.15625
- pairs: int32 [128, 3], P('ka'), may hold values from 0 to 31, as said below
- q_slot: int32 [16], replicated, may hold values from 0 to 15, as said below
Outputs:
- blocks: float32 [128, 4096], P('ka')
- mirrored: float32 [32, 4096], P('ka')
Inputs may be any that keep to these rules, and one draw needn't show every extreme that they name: `pairs`: column 0 of the rows held by index d of ka lies in d * 4 to (d + 1) * 4 - 1; column 1 is any k-point; column 2 is a momentum transfer below 16. Among one index's 16 rows at most 2 have a second k-point held by one same index, and this is reached; at most 2 have q_slot[q] // 2 equal to one same value, and this is reached. `q_slot`: A permutation of the slots; slot s of screened is held by index s // 2 of ka.
All inputs are finite; a program needn't handle non-finite values.
Results may differ from a plain program's by a relative error of at most 0.0014.
Values may be sent and summed in bfloat16 or wider, within the bound.
A program may use at most 192 MiB of HBM per device.

v0:
```python
import jax
import jax.numpy as jnp
from jax import lax
from jax.sharding import PartitionSpec as P

CAPQ = 2
CAPK = 2


def earlier_count(owners):
    places = jnp.arange(owners.shape[0])
    same_owner = owners[:, None] == owners[None, :]
    before = places[:, None] > places[None, :]
    return jnp.sum(jnp.logical_and(same_owner, before).astype(jnp.int32), axis=1)


def per_device(x_dens, y_dens, p_dens, coulomb, screened, pairs, q_slot):
    n_ka = lax.axis_size("ka")
    mine_index = lax.axis_index("ka")
    per_dev, transitions, g_local = x_dens.shape
    q_slots = screened.shape[0]
    pair_rows = pairs.shape[0]
    k_local = pairs[:, 0] - mine_index * per_dev
    partner = pairs[:, 1]
    q_index = pairs[:, 2]
    slot_of = jnp.sum(
        jnp.where(q_index[:, None] == jnp.arange(q_slot.shape[0])[None, :], q_slot[None, :], 0),
        axis=1,
    )
    q_owner = slot_of // q_slots
    q_local = slot_of % q_slots
    q_rank = earlier_count(q_owner)
    q_route = ((q_owner * CAPQ + q_rank)[:, None] == jnp.arange(n_ka * CAPQ)[None, :]).astype(
        jnp.bfloat16
    )
    pick_first = (k_local[:, None] == jnp.arange(per_dev)[None, :]).astype(jnp.bfloat16)
    x_rows = jnp.einsum(
        "jk,kig->jig", pick_first, x_dens, preferred_element_type=jnp.float32
    ).astype(jnp.bfloat16)
    p_rows = jnp.einsum(
        "jk,kig->jig", pick_first, p_dens, preferred_element_type=jnp.float32
    ).astype(jnp.bfloat16)
    send_x = jnp.einsum("js,jig->sig", q_route, x_rows, preferred_element_type=jnp.float32).astype(
        jnp.bfloat16
    )
    send_x = send_x.reshape(n_ka, CAPQ, transitions, g_local)
    send_q = jnp.sum(q_route.astype(jnp.int32) * q_local[:, None], axis=0).reshape(n_ka, CAPQ)
    got_x, got_q = (
        lax.all_to_all(send_x, "ka", split_axis=0, concat_axis=0, tiled=True),
        lax.all_to_all(send_q, "ka", split_axis=0, concat_axis=0, tiled=True),
    )
    chosen = (got_q[:, :, None] == jnp.arange(q_slots)[None, None, :]).astype(jnp.bfloat16)
    stacked = got_x[:, :, None, :, :] * chosen[:, :, :, None, None]
    partial_value = jnp.einsum(
        "ncsig,sgh->hnci", stacked, screened, preferred_element_type=jnp.float32
    )
    half_rows = lax.psum_scatter(
        partial_value.reshape(lax.axis_size("ga") * g_local, n_ka, CAPQ * transitions),
        "ga",
        scatter_dimension=0,
        tiled=True,
    ).astype(jnp.bfloat16)
    returned = lax.all_to_all(half_rows, "ka", split_axis=1, concat_axis=1, tiled=True)
    returned = returned.reshape(g_local, n_ka * CAPQ, transitions)
    u_rows = jnp.einsum(
        "js,gsi->jig", q_route, returned, preferred_element_type=jnp.float32
    ).astype(jnp.bfloat16)
    all_pairs = lax.all_gather(pairs, "ka", axis=0, tiled=True).reshape(n_ka, pair_rows, 3)
    seconds = all_pairs[:, :, 1]
    k_owners = seconds // per_dev
    k_ranks = jax.vmap(earlier_count)(k_owners)
    held_here = k_owners == mine_index
    rank_hot = (k_ranks[:, :, None] == jnp.arange(CAPK)[None, None, :]).astype(jnp.float32)
    local_hot = jnp.logical_and(
        (seconds - mine_index * per_dev)[:, :, None] == jnp.arange(per_dev)[None, None, :],
        held_here[:, :, None],
    ).astype(jnp.float32)
    selector = jnp.einsum("njc,njk->nck", rank_hot, local_hot).astype(jnp.bfloat16)
    send_y = jnp.einsum(
        "nck,kig->ncig", selector, y_dens, preferred_element_type=jnp.float32
    ).astype(jnp.bfloat16)
    send_p = jnp.einsum(
        "nck,kig->ncig", selector, p_dens, preferred_element_type=jnp.float32
    ).astype(jnp.bfloat16)
    got_y, got_p = (
        lax.all_to_all(send_y, "ka", split_axis=0, concat_axis=0, tiled=True),
        lax.all_to_all(send_p, "ka", split_axis=0, concat_axis=0, tiled=True),
    )
    own_rank = earlier_count(partner // per_dev)
    pick_second = (
        (partner // per_dev * CAPK + own_rank)[:, None] == jnp.arange(n_ka * CAPK)[None, :]
    ).astype(jnp.bfloat16)
    y_rows = jnp.einsum(
        "js,sig->jig",
        pick_second,
        got_y.reshape(n_ka * CAPK, transitions, g_local),
        preferred_element_type=jnp.float32,
    ).astype(jnp.bfloat16)
    pp_rows = jnp.einsum(
        "js,sig->jig",
        pick_second,
        got_p.reshape(n_ka * CAPK, transitions, g_local),
        preferred_element_type=jnp.float32,
    ).astype(jnp.bfloat16)
    direct = jnp.einsum("jig,jhg->jih", u_rows, y_rows, preferred_element_type=jnp.float32)
    weighted = p_rows.astype(jnp.float32) * coulomb[None, None, :]
    exchange_term = jnp.einsum(
        "jig,jhg->jih", weighted, pp_rows.astype(jnp.float32), precision=lax.Precision.HIGHEST
    )
    kernel_block = lax.psum(2.0 * exchange_term - direct, "ga")
    blocks = kernel_block.reshape(pair_rows, transitions * transitions)
    flipped = jnp.transpose(kernel_block, (0, 2, 1)).reshape(pair_rows, transitions * transitions)
    selector = (partner[:, None] == jnp.arange(lax.axis_size("ka") * per_dev)[None, :]).astype(
        jnp.float32
    )
    mirrored = lax.psum_scatter(
        jnp.dot(selector.T, flipped, precision=lax.Precision.HIGHEST),
        "ka",
        scatter_dimension=0,
        tiled=True,
    )
    return (blocks, mirrored)


def solution(mesh):
    in_specs = (
        P("ka", None, "ga"),
        P("ka", None, "ga"),
        P("ka", None, "ga"),
        P("ga"),
        P("ka", "ga", None),
        P("ka", None),
        P(),
    )
    out_specs = (P("ka", None), P("ka", None))
    return jax.shard_map(
        per_device, mesh=mesh, in_specs=in_specs, out_specs=out_specs, check_vma=False
    )
```

profile of v0, /device:TPU:0, one launch (start us, length us, event | category | flops | bytes accessed | tf_op | source)
XLA Modules:
  0.0 274.0 jit_solution(15575906817718074861)
XLA Ops:
  9.9 7.3 %all-to-all-start.2 = ((s32[8,1,2]{2,1,0:T(1,128)}), s32[8,1,2]{2,1,0:T(1,128)S(1)}, u32[]{:S(2)}, u32[]{:S(2)}) async-start(s32[8,1,2]{2,1,0:T(1,128)} %bitcast.18), calls=%async_computation.2 | async-start | bytes 8192 | tf_op jit(solution)/shard_map/all_to_all | solution.py:50
  17.2 2.5 convolution_convert_fusion.3
  19.7 2.2 reshape.166
  21.9 1.5 copy.117
  23.6 5.8 %all-to-all-start.1 = ((bf16[8,2,64,375]{3,1,2,0:T(2,128)(2,1)}), bf16[8,2,64,375]{3,1,2,0:T(2,128)(2,1)S(1)}, u32[]{:S(2)}, u32[]{:S(2)}) async-start(bf16[8,2,64,375]{3,1,2,0:T(2,128)(2,1)} %copy.117), calls=%async_computation.1 | async-start | bytes 1572864 | tf_op jit(solution)/shard_map/all_to_all | solution.py:49
  29.5 19.6 %all-to-all-done.1 = bf16[8,2,64,375]{3,1,2,0:T(2,128)(2,1)S(1)} async-done(((bf16[8,2,64,375]{3,1,2,0:T(2,128)(2,1)}), bf16[8,2,64,375]{3,1,2,0:T(2,128)(2,1)S(1)}, u32[]{:S(2)}, u32[]{:S(2)}) %all-to-all-start.1) | async-done | bytes 768032 | tf_op jit(solution)/shard_map/all_to_all | solution.py:49
  49.2 5.0 %fusion = f32[8,2,64,1500,1]{3,2,4,1,0:T(8,128)} fusion(bf16[2,375,1500,1,1]{2,0,1,4,3:T(2,128)(2,1)S(1)} %bitcast.72, bf16[8,2,2]{2,1,0:T(2,128)(2,1)S(1)} %compare_convert_fusion, bf16[8,2,64,375]{3,2,1,0:T(8,128)(2,1)S(1)} %copy.118), kind=kOutput, calls=%fused_computation | convolution fusion | flops 2304768000 | bytes 9162064 | tf_op jit(solution)/shard_map/ncsig,sgh->hnci/dot_general | solution.py:54
  54.2 6.5 %copy.123 = f32[1500,8,128]{2,1,0:T(8,128)} copy(f32[1500,8,128]{0,2,1:T(8,128)} %bitcast.73) | data formatting | bytes 12288000 | tf_op jit(solution)/shard_map/reshape | solution.py:58
  61.4 26.1 %all-gather = s32[8,16,3]{1,2,0:T(4,128)S(1)} all-gather(s32[1,16,3]{1,2,0:T(4,128)S(1)} %bitcast.81), channel_id=1, replica_groups=mesh['ka'=8,'ga'=4] {'ka'}, dimensions={0}, use_global_device_ids=true | all-gather | bytes 1728 | tf_op jit(solution)/shard_map/all_gather | solution.py:68
  89.6 3.5 %all-to-all-start = ((bf16[8,2,64,375]{3,2,1,0:T(8,128)(2,1)}), bf16[8,2,64,375]{3,2,1,0:T(8,128)(2,1)S(1)}, u32[]{:S(2)}, u32[]{:S(2)}) async-start(bf16[8,2,64,375]{3,2,1,0:T(8,128)(2,1)} %copy.111), calls=%async_computation | async-start | bytes 1572864 | tf_op jit(solution)/shard_map/all_to_all | solution.py:87
  94.6 13.4 %all-to-all-done = bf16[8,2,64,375]{3,2,1,0:T(8,128)(2,1)S(1)} async-done(((bf16[8,2,64,375]{3,2,1,0:T(8,128)(2,1)}), bf16[8,2,64,375]{3,2,1,0:T(8,128)(2,1)S(1)}, u32[]{:S(2)}, u32[]{:S(2)}) %all-to-all-start) | async-done | bytes 768032 | tf_op jit(solution)/shard_map/all_to_all | solution.py:87
  108.0 4.2 %all-to-all-start.4 = ((bf16[8,2,64,375]{3,2,1,0:T(8,128)(2,1)}), bf16[8,2,64,375]{3,2,1,0:T(8,128)(2,1)}, u32[]{:S(2)}, u32[]{:S(2)}) async-start(bf16[8,2,64,375]{3,2,1,0:T(8,128)(2,1)} %copy.128), calls=%async_computation.4 | async-start | bytes 1572864 | tf_op jit(solution)/shard_map/all_to_all | solution.py:86
  112.2 5.5 %reduce-scatter.4.cloned.1.call-done = f32[375,8,128]{2,1,0:T(8,128)} async-done(((f32[1500,8,128]{2,1,0:T(8,128)}), f32[375,8,128]{2,1,0:T(8,128)}) %reduce-scatter.4.cloned.1.call-update) | async-done | bytes 1536016
  117.7 1.5 convert_element_type.77
  120.1 9.4 %all-to-all-done.4 = bf16[8,2,64,375]{3,2,1,0:T(8,128)(2,1)} async-done(((bf16[8,2,64,375]{3,2,1,0:T(8,128)(2,1)}), bf16[8,2,64,375]{3,2,1,0:T(8,128)(2,1)}, u32[]{:S(2)}, u32[]{:S(2)}) %all-to-all-start.4) | async-done | bytes 768032 | tf_op jit(solution)/shard_map/all_to_all | solution.py:86
  129.5 4.2 %all-to-all-start.3 = ((bf16[375,8,128]{2,0,1:T(8,128)(2,1)}), bf16[375,8,128]{2,0,1:T(8,128)(2,1)}, u32[]{:S(2)}, u32[]{:S(2)}) async-start(bf16[375,8,128]{2,0,1:T(8,128)(2,1)} %copy.124), calls=%async_computation.3 | async-start | bytes 1540096 | tf_op jit(solution)/shard_map/all_to_all | solution.py:63
  135.0 2.6 convolution_convert_fusion
  137.7 2.3 fusion.6
  140.0 12.0 %all-to-all-done.3 = bf16[375,8,128]{2,0,1:T(8,128)(2,1)} async-done(((bf16[375,8,128]{2,0,1:T(8,128)(2,1)}), bf16[375,8,128]{2,0,1:T(8,128)(2,1)}, u32[]{:S(2)}, u32[]{:S(2)}) %all-to-all-start.3) | async-done | bytes 768032 | tf_op jit(solution)/shard_map/all_to_all | solution.py:63
  152.0 1.5 copy.125
  156.0 32.5 %all-reduce.5.cloned.1.call-done = f32[16,64,64]{2,1,0:T(8,128)} async-done(((f32[16,64,64]{2,1,0:T(8,128)}), f32[16,64,64]{2,1,0:T(8,128)}) %all-reduce.5.cloned.1.call-update) | async-done | bytes 262160 | tf_op jit(solution)/shard_map/psum | solution.py:110
  190.7 2.2 fusion.37
  195.1 70.8 %all-reduce.7.cloned.1.call-done = f32[32,4096]{1,0:T(8,128)} async-done(((f32[32,4096]{1,0:T(8,128)}), f32[32,4096]{1,0:T(8,128)}) %all-reduce.7.cloned.1.call-update) | async-done | bytes 524304
  265.9 1.5 constant_dynamic-slice_fusion
  (58 shorter events, 15.8 us)
Async XLA Ops:
  7.2 42.0 %copy-start = (bf16[2,375,1500]{2,0,1:T(2,128)(2,1)S(1)}, bf16[2,375,1500]{2,0,1:T(2,128)(2,1)}, u32[]{:S(2)}) copy-start(bf16[2,375,1500]{2,0,1:T(2,128)(2,1)} %param.11) | copy-start | bytes 6750004
  9.9 13.7 %all-to-all-start.2 = ((s32[8,1,2]{2,1,0:T(1,128)}), s32[8,1,2]{2,1,0:T(1,128)S(1)}, u32[]{:S(2)}, u32[]{:S(2)}) async-start(s32[8,1,2]{2,1,0:T(1,128)} %bitcast.18), calls=%async_computation.2 | async-start | bytes 8192 | tf_op jit(solution)/shard_map/all_to_all | solution.py:50
  23.6 25.5 %all-to-all-start.1 = ((bf16[8,2,64,375]{3,1,2,0:T(2,128)(2,1)}), bf16[8,2,64,375]{3,1,2,0:T(2,128)(2,1)S(1)}, u32[]{:S(2)}, u32[]{:S(2)}) async-start(bf16[8,2,64,375]{3,1,2,0:T(2,128)(2,1)} %copy.117), calls=%async_computation.1 | async-start | bytes 1572864 | tf_op jit(solution)/shard_map/all_to_all | solution.py:49
  29.4 88.3 %reduce-scatter.4.cloned.1.call-start = ((), (), s32[]{:S(2)}) async-start(), calls=%async_computation.8 | async-start | bytes 7680000
  60.7 0.7 copy-start.6
  60.7 27.4 %copy-start.4 = (bf16[4,64,375]{2,1,0:T(8,128)(2,1)S(1)}, bf16[4,64,375]{2,1,0:T(8,128)(2,1)}, u32[]{:S(2)}) copy-start(bf16[4,64,375]{2,1,0:T(8,128)(2,1)} %param.9) | copy-start | bytes 576004
  88.5 4.6 %copy-start.5 = (bf16[4,64,375]{2,1,0:T(8,128)(2,1)S(1)}, bf16[4,64,375]{2,1,0:T(8,128)(2,1)}, u32[]{:S(2)}) copy-start(bf16[4,64,375]{2,1,0:T(8,128)(2,1)} %param.8) | copy-start | bytes 576004
  89.6 18.4 %all-to-all-start = ((bf16[8,2,64,375]{3,2,1,0:T(8,128)(2,1)}), bf16[8,2,64,375]{3,2,1,0:T(8,128)(2,1)S(1)}, u32[]{:S(2)}, u32[]{:S(2)}) async-start(bf16[8,2,64,375]{3,2,1,0:T(8,128)(2,1)} %copy.111), calls=%async_computation | async-start | bytes 1572864 | tf_op jit(solution)/shard_map/all_to_all | solution.py:87
  108.0 21.6 %all-to-all-start.4 = ((bf16[8,2,64,375]{3,2,1,0:T(8,128)(2,1)}), bf16[8,2,64,375]{3,2,1,0:T(8,128)(2,1)}, u32[]{:S(2)}, u32[]{:S(2)}) async-start(bf16[8,2,64,375]{3,2,1,0:T(8,128)(2,1)} %copy.128), calls=%async_computation.4 | async-start | bytes 1572864 | tf_op jit(solution)/shard_map/all_to_all | solution.py:86
  119.1 14.9 %copy-start.7 = (f32[375]{0:T(512)S(1)}, f32[375]{0:T(512)}, u32[]{:S(2)}) copy-start(f32[375]{0:T(512)} %param.10) | copy-start | bytes 4504
  129.5 22.4 %all-to-all-start.3 = ((bf16[375,8,128]{2,0,1:T(8,128)(2,1)}), bf16[375,8,128]{2,0,1:T(8,128)(2,1)}, u32[]{:S(2)}, u32[]{:S(2)}) async-start(bf16[375,8,128]{2,0,1:T(8,128)(2,1)} %copy.124), calls=%async_computation.3 | async-start | bytes 1540096 | tf_op jit(solution)/shard_map/all_to_all | solution.py:63
  133.7 54.8 %all-reduce.5.cloned.1.call-start = ((), (), s32[]{:S(2)}) async-start(), calls=%async_computation.6 | async-start | bytes 1048576 | tf_op jit(solution)/shard_map/psum | solution.py:110
  153.5 1.1 copy-start.1
  153.5 1.3 copy-start.3
  156.0 109.9 %all-reduce.7.cloned.1.call-start = ((), (), s32[]{:S(2)}) async-start(), calls=%async_computation.7 | async-start | bytes 1048576
  188.5 4.5 %copy-start.8 = (u32[32]{0:T(128)S(1)}, u32[32]{0:T(128)}, u32[]{:S(2)}) copy-start(u32[32]{0:T(128)} %constant.69) | copy-start | bytes 388
  188.5 5.7 %copy-start.2 = (f32[16,64,64]{2,1,0:T(8,128)S(1)}, f32[16,64,64]{2,1,0:T(8,128)}, u32[]{:S(2)}) copy-start(f32[16,64,64]{2,1,0:T(8,128)} %all-reduce.5.cloned.1.call-done) | copy-start | bytes 786436
Sparse Core Ops, SparseCore 0:
  60.9 56.7 reduce-scatter.3
  156.1 32.3 all-reduce.4
  193.1 72.7 all-reduce.6
where the time goes:
time: 275 us; the launch traced here: 274 us
  waiting for transfers between devices  163 us (59%)
  blocking collectives  26.1 us (9%)
  starting transfers between devices  25.2 us (9%)
  local copies, waits for them, and re-layouts  22.1 us (8%)
  matrix products  18.5 us (7%)
  between operations  14.6 us (5%)
  other arithmetic  4.08 us (1%)
    unnamed x5, waiting for transfers between devices  76.3 us
    psum x1, waiting for transfers between devices, per_device(): kernel_block = lax.psum(2.0 * exchange_term - direct, 'ga')  32.5 us
    all_gather x1, blocking collectives, per_device(): lax.all_gather(pairs, 'ka', axis=0, tiled=True).reshape(n_ka, pair_rows, 3)  26.1 us
    all_to_all x1, waiting for transfers between devices, per_device(): lax.all_to_all(send_x, 'ka', split_axis=0, concat_axis=0, tiled=True)  19.6 us
    all_to_all x1, waiting for transfers between devices, per_device(): lax.all_to_all(send_p, 'ka', split_axis=0, concat_axis=0, tiled=True)  13.4 us
    all_to_all x1, waiting for transfers between devices, per_device(): lax.all_to_all(half_rows, 'ka', split_axis=1, concat_axis=1, tiled=True)  12 us
    all_to_all x1, waiting for transfers between devices, per_device(): lax.all_to_all(send_y, 'ka', split_axis=0, concat_axis=0, tiled=True)  9.42 us
    all_to_all x1, starting transfers between devices, per_device(): lax.all_to_all(send_q, 'ka', split_axis=0, concat_axis=0, tiled=True)  7.31 us
  transfers between devices with their start and end apart: 8, of which 8 were waited for; matrix products, arithmetic and copies ran while one was open for 7% of the time, Pallas kernels for 0%

commit v1 on v0

--- a/solution.py
+++ b/solution.py
@@ -60,7 +60,10 @@
         scatter_dimension=0,
         tiled=True,
     ).astype(jnp.bfloat16)
-    returned = lax.all_to_all(half_rows, "ka", split_axis=1, concat_axis=1, tiled=True)
+    returned = jnp.concatenate(
+        lax.all_to_all(jnp.stack(jnp.split(half_rows, lax.axis_size("ka"), axis=1)), "ka", 0, 0),
+        axis=1,
+    )
     returned = returned.reshape(g_local, n_ka * CAPQ, transitions)
     u_rows = jnp.einsum(
         "js,gsi->jig", q_route, returned, preferred_element_type=jnp.float32

time: 275 us -> 292 us (1.062)
  local copies, waits for them, and re-layouts: 22.1 us -> 33.6 us
  waiting for transfers between devices: 163 us -> 169 us
    unnamed x5, waiting for transfers between devices: 76.3 us -> 93.9 us
    all_to_all x1, waiting for transfers between devices: 13.4 us -> 0.01 us  [per_device(): lax.all_to_all(send_p, 'ka', split_axis=0, concat_axis=0, tiled=True)]
    unnamed x20 -> x29, local copies, waits for them, and re-layouts: 3.49 us -> 12.7 us
  transfers between devices with their start and end apart: 8 -> 8, of which waited for: 8 -> 7; matrix products, arithmetic and copies ran while one was open for 7% -> 10% of each run, Pallas kernels for 0% -> 0%
where the time goes in v1:
time: 292 us; the launch traced here: 291 us
  waiting for transfers between devices  169 us (58%)
  local copies, waits for them, and re-layouts  33.6 us (12%)
  starting transfers between devices  26.5 us (9%)
  blocking collectives  26.1 us (9%)
  matrix products  18.5 us (6%)
  between operations  14.6 us (5%)
    unnamed x5, waiting for transfers between devices  93.9 us
    psum x1, waiting for transfers between devices, per_device(): kernel_block = lax.psum(2.0 * exchange_term - direct, 'ga')  31.5 us
    all_gather x1, blocking collectives, per_device(): lax.all_gather(pairs, 'ka', axis=0, tiled=True).reshape(n_ka, pair_rows, 3)  26.1 us
    all_to_all x1, waiting for transfers between devices, per_device(): lax.all_to_all(send_x, 'ka', split_axis=0, concat_axis=0, tiled=True)  19.6 us
    all_to_all x1, waiting for transfers between devices, per_device(): lax.all_to_all(jnp.stack(jnp.split(half_rows, lax.axis_size('ka'), axis=1...  13.2 us
    unnamed x29, local copies, waits for them, and re-layouts  12.7 us
    all_to_all x1, waiting for transfers between devices, per_device(): lax.all_to_all(send_y, 'ka', split_axis=0, concat_axis=0, tiled=True)  11 us
    all_to_all x1, starting transfers between devices, per_device(): lax.all_to_all(send_q, 'ka', split_axis=0, concat_axis=0, tiled=True)  7.31 us
  transfers between devices with their start and end apart: 8, of which 7 were waited for; matrix products, arithmetic and copies ran while one was open for 10% of the time, Pallas kernels for 0%

profile of v1, /device:TPU:0, one launch (start us, length us, event | category | flops | bytes accessed | tf_op | source)
XLA Modules:
  0.0 291.2 jit_solution(9597512237130209519)
XLA Ops:
  9.9 7.3 %all-to-all-start.2 = ((s32[8,1,2]{2,1,0:T(1,128)}), s32[8,1,2]{2,1,0:T(1,128)S(1)}, u32[]{:S(2)}, u32[]{:S(2)}) async-start(s32[8,1,2]{2,1,0:T(1,128)} %bitcast.18), calls=%async_computation.2 | async-start | bytes 8192 | tf_op jit(solution)/shard_map/all_to_all | solution.py:50
  17.2 2.5 convolution_convert_fusion.3
  19.7 2.2 reshape.166
  23.6 5.8 %all-to-all-start.1 = ((bf16[8,2,64,375]{3,1,2,0:T(2,128)(2,1)}), bf16[8,2,64,375]{3,1,2,0:T(2,128)(2,1)S(1)}, u32[]{:S(2)}, u32[]{:S(2)}) async-start(bf16[8,2,64,375]{3,1,2,0:T(2,128)(2,1)} %copy.123), calls=%async_computation.1 | async-start | bytes 1572864 | tf_op jit(solution)/shard_map/all_to_all | solution.py:49
  29.5 19.6 %all-to-all-done.1 = bf16[8,2,64,375]{3,1,2,0:T(2,128)(2,1)S(1)} async-done(((bf16[8,2,64,375]{3,1,2,0:T(2,128)(2,1)}), bf16[8,2,64,375]{3,1,2,0:T(2,128)(2,1)S(1)}, u32[]{:S(2)}, u32[]{:S(2)}) %all-to-all-start.1) | async-done | bytes 768032 | tf_op jit(solution)/shard_map/all_to_all | solution.py:49
  49.2 4.9 %fusion = f32[8,2,64,1500,1]{3,2,4,1,0:T(8,128)} fusion(bf16[2,375,1500,1,1]{2,0,1,4,3:T(2,128)(2,1)S(1)} %bitcast.106, bf16[8,2,2]{2,1,0:T(2,128)(2,1)S(1)} %compare_convert_fusion, bf16[8,2,64,375]{3,2,1,0:T(8,128)(2,1)S(1)} %copy.124), kind=kOutput, calls=%fused_computation | convolution fusion | flops 2304768000 | bytes 9162064 | tf_op jit(solution)/shard_map/ncsig,sgh->hnci/dot_general | solution.py:54
  54.1 6.5 %copy.129 = f32[1500,8,128]{2,1,0:T(8,128)} copy(f32[1500,8,128]{0,2,1:T(8,128)} %bitcast.107) | data formatting | bytes 12288000 | tf_op jit(solution)/shard_map/reshape | solution.py:58
  61.3 26.1 %all-gather = s32[8,16,3]{1,2,0:T(4,128)S(1)} all-gather(s32[1,16,3]{1,2,0:T(4,128)S(1)} %bitcast.115), channel_id=1, replica_groups=mesh['ka'=8,'ga'=4] {'ka'}, dimensions={0}, use_global_device_ids=true | all-gather | bytes 1728 | tf_op jit(solution)/shard_map/all_gather | solution.py:71
  89.5 3.5 %all-to-all-start = ((bf16[8,2,64,375]{3,2,1,0:T(8,128)(2,1)}), bf16[8,2,64,375]{3,2,1,0:T(8,128)(2,1)S(1)}, u32[]{:S(2)}, u32[]{:S(2)}) async-start(bf16[8,2,64,375]{3,2,1,0:T(8,128)(2,1)} %copy.117), calls=%async_computation | async-start | bytes 1572864 | tf_op jit(solution)/shard_map/all_to_all | solution.py:90
  94.5 23.1 %reduce-scatter.4.cloned.1.call-done = f32[375,8,128]{2,1,0:T(8,128)} async-done(((f32[1500,8,128]{2,1,0:T(8,128)}), f32[375,8,128]{2,1,0:T(8,128)}) %reduce-scatter.4.cloned.1.call-update) | async-done | bytes 1536016
  117.6 1.7 copy.180
  120.8 5.5 %all-to-all-start.4 = ((bf16[8,2,64,375]{3,2,1,0:T(8,128)(2,1)}), bf16[8,2,64,375]{3,2,1,0:T(8,128)(2,1)}, u32[]{:S(2)}, u32[]{:S(2)}) async-start(bf16[8,2,64,375]{3,2,1,0:T(8,128)(2,1)} %copy.134), calls=%async_computation.4 | async-start | bytes 1572864 | tf_op jit(solution)/shard_map/all_to_all | solution.py:89
  129.4 1.5 fusion.27
  132.5 1.5 fusion.25
  134.0 1.5 fusion.24
  135.6 11.0 %all-to-all-done.4 = bf16[8,2,64,375]{3,2,1,0:T(8,128)(2,1)} async-done(((bf16[8,2,64,375]{3,2,1,0:T(8,128)(2,1)}), bf16[8,2,64,375]{3,2,1,0:T(8,128)(2,1)}, u32[]{:S(2)}, u32[]{:S(2)}) %all-to-all-start.4) | async-done | bytes 768032 | tf_op jit(solution)/shard_map/all_to_all | solution.py:89
  146.5 4.2 %all-to-all-start.3 = ((bf16[8,375,1,128]{3,1,2,0:T(8,128)(2,1)}), bf16[8,375,1,128]{3,1,2,0:T(8,128)(2,1)}, u32[]{:S(2)}, u32[]{:S(2)}) async-start(bf16[8,375,1,128]{3,1,2,0:T(8,128)(2,1)} %fusion.24), calls=%async_computation.3 | async-start | bytes 1540096 | tf_op jit(solution)/shard_map/all_to_all | solution.py:64
  152.1 2.6 convolution_convert_fusion
  154.7 2.3 fusion.6
  157.0 13.2 %all-to-all-done.3 = bf16[8,375,1,128]{3,1,2,0:T(8,128)(2,1)} async-done(((bf16[8,375,1,128]{3,1,2,0:T(8,128)(2,1)}), bf16[8,375,1,128]{3,1,2,0:T(8,128)(2,1)}, u32[]{:S(2)}, u32[]{:S(2)}) %all-to-all-start.3) | async-done | bytes 768032 | tf_op jit(solution)/shard_map/all_to_all | solution.py:64
  174.3 31.5 %all-reduce.5.cloned.1.call-done = f32[16,64,64]{2,1,0:T(8,128)} async-done(((f32[16,64,64]{2,1,0:T(8,128)}), f32[16,64,64]{2,1,0:T(8,128)}) %all-reduce.5.cloned.1.call-update) | async-done | bytes 262160 | tf_op jit(solution)/shard_map/psum | solution.py:113
  208.0 2.2 fusion.45
  212.4 70.8 %all-reduce.7.cloned.1.call-done = f32[32,4096]{1,0:T(8,128)} async-done(((f32[32,4096]{1,0:T(8,128)}), f32[32,4096]{1,0:T(8,128)}) %all-reduce.7.cloned.1.call-update) | async-done | bytes 524304
  283.2 1.5 constant_dynamic-slice_fusion
  (67 shorter events, 23.9 us)
Async XLA Ops:
  7.2 42.1 %copy-start = (bf16[2,375,1500]{2,0,1:T(2,128)(2,1)S(1)}, bf16[2,375,1500]{2,0,1:T(2,128)(2,1)}, u32[]{:S(2)}) copy-start(bf16[2,375,1500]{2,0,1:T(2,128)(2,1)} %param.11) | copy-start | bytes 6750004
  9.9 13.7 %all-to-all-start.2 = ((s32[8,1,2]{2,1,0:T(1,128)}), s32[8,1,2]{2,1,0:T(1,128)S(1)}, u32[]{:S(2)}, u32[]{:S(2)}) async-start(s32[8,1,2]{2,1,0:T(1,128)} %bitcast.18), calls=%async_computation.2 | async-start | bytes 8192 | tf_op jit(solution)/shard_map/all_to_all | solution.py:50
  23.6 25.5 %all-to-all-start.1 = ((bf16[8,2,64,375]{3,1,2,0:T(2,128)(2,1)}), bf16[8,2,64,375]{3,1,2,0:T(2,128)(2,1)S(1)}, u32[]{:S(2)}, u32[]{:S(2)}) async-start(bf16[8,2,64,375]{3,1,2,0:T(2,128)(2,1)} %copy.123), calls=%async_computation.1 | async-start | bytes 1572864 | tf_op jit(solution)/shard_map/all_to_all | solution.py:49
  29.4 88.2 %reduce-scatter.4.cloned.1.call-start = ((), (), s32[]{:S(2)}) async-start(), calls=%async_computation.8 | async-start | bytes 7680000
  60.6 0.7 copy-start.7
  60.6 27.4 %copy-start.5 = (bf16[4,64,375]{2,1,0:T(8,128)(2,1)S(1)}, bf16[4,64,375]{2,1,0:T(8,128)(2,1)}, u32[]{:S(2)}) copy-start(bf16[4,64,375]{2,1,0:T(8,128)(2,1)} %param.9) | copy-start | bytes 576004
  88.5 4.6 %copy-start.6 = (bf16[4,64,375]{2,1,0:T(8,128)(2,1)S(1)}, bf16[4,64,375]{2,1,0:T(8,128)(2,1)}, u32[]{:S(2)}) copy-start(bf16[4,64,375]{2,1,0:T(8,128)(2,1)} %param.8) | copy-start | bytes 576004
  89.5 31.4 %all-to-all-start = ((bf16[8,2,64,375]{3,2,1,0:T(8,128)(2,1)}), bf16[8,2,64,375]{3,2,1,0:T(8,128)(2,1)S(1)}, u32[]{:S(2)}, u32[]{:S(2)}) async-start(bf16[8,2,64,375]{3,2,1,0:T(8,128)(2,1)} %copy.117), calls=%async_computation | async-start | bytes 1572864 | tf_op jit(solution)/shard_map/all_to_all | solution.py:90
  119.3 0.9 copy-start.2
  120.8 25.7 %all-to-all-start.4 = ((bf16[8,2,64,375]{3,2,1,0:T(8,128)(2,1)}), bf16[8,2,64,375]{3,2,1,0:T(8,128)(2,1)}, u32[]{:S(2)}, u32[]{:S(2)}) async-start(bf16[8,2,64,375]{3,2,1,0:T(8,128)(2,1)} %copy.134), calls=%async_computation.4 | async-start | bytes 1572864 | tf_op jit(solution)/shard_map/all_to_all | solution.py:89
  126.4 24.6 %copy-start.8 = (f32[375]{0:T(512)S(1)}, f32[375]{0:T(512)}, u32[]{:S(2)}) copy-start(f32[375]{0:T(512)} %param.10) | copy-start | bytes 4504
  146.5 23.7 %all-to-all-start.3 = ((bf16[8,375,1,128]{3,1,2,0:T(8,128)(2,1)}), bf16[8,375,1,128]{3,1,2,0:T(8,128)(2,1)}, u32[]{:S(2)}, u32[]{:S(2)}) async-start(bf16[8,375,1,128]{3,1,2,0:T(8,128)(2,1)} %fusion.24), calls=%async_computation.3 | async-start | bytes 1540096 | tf_op jit(solution)/shard_map/all_to_all | solution.py:64
  150.8 55.0 %all-reduce.5.cloned.1.call-start = ((), (), s32[]{:S(2)}) async-start(), calls=%async_computation.6 | async-start | bytes 1048576 | tf_op jit(solution)/shard_map/psum | solution.py:113
  171.7 1.1 copy-start.1
  171.7 1.3 copy-start.4
  174.2 109.0 %all-reduce.7.cloned.1.call-start = ((), (), s32[]{:S(2)}) async-start(), calls=%async_computation.7 | async-start | bytes 1048576
  205.8 4.5 %copy-start.9 = (u32[32]{0:T(128)S(1)}, u32[32]{0:T(128)}, u32[]{:S(2)}) copy-start(u32[32]{0:T(128)} %constant.69) | copy-start | bytes 388
  205.8 5.7 %copy-start.3 = (f32[16,64,64]{2,1,0:T(8,128)S(1)}, f32[16,64,64]{2,1,0:T(8,128)}, u32[]{:S(2)}) copy-start(f32[16,64,64]{2,1,0:T(8,128)} %all-reduce.5.cloned.1.call-done) | copy-start | bytes 786436
Sparse Core Ops, SparseCore 0:
  60.8 56.7 reduce-scatter.3
  174.3 31.3 all-reduce.4
  210.4 72.7 all-reduce.6
